TPU v7x, 32 devices: a whole 2x2x4 slice. The times are simulated.
32 devices in a mesh: dp: 16 (over z, y, x), rep: 2 (over core).
Axes of the slice: x: 2, y: 2, z: 4, core: 2. Of those that a mesh axis runs over, the one named last changes fastest.
Arguments:
- queries: bfloat16 [2048, 2048], P(('dp', 'rep')), may hold values from -24 to 24
- documents: bfloat16 [2048, 2048], P(('dp', 'rep')), may hold values from -24 to 24
- partner: int32 [2048], P(('dp', 'rep')), may hold values from 0 to 2047, each once
Outputs:
- grad_queries: float32 [2048, 2048], P(('dp', 'rep'))
- grad_documents: float32 [2048, 2048], P(('dp', 'rep'))
Inputs may be any that keep to these rules, and one draw needn't show every extreme that they name: `partner`: every document index appears exactly once.
All inputs are finite; a program needn't handle non-finite values.
Results may differ from a plain program's by a relative error of at most 0.0031.
Values may be sent and summed in bfloat16 or wider, within the bound.
No kernel may reach another device: no remote copies, remote signals or barrier semaphores. Data moves between devices by JAX's collectives and lax.ppermute only.
A program may use at most 256 MiB of HBM per device.

v0:
```python
import jax
import jax.numpy as jnp
from jax import lax
from jax.sharding import PartitionSpec as P

WIDTHS = 9
logit_gain = 3.0


def merged(x, axis, combine):
    everything = jax.tree.map(lambda part: lax.all_gather(part, axis), x)
    leading = jax.tree.map(lambda part: part[0], everything)

    def hop(k, so_far):
        return combine(so_far, jax.tree.map(lambda part: part[k], everything))

    return lax.fori_loop(1, lax.axis_size(axis), hop, leading)


def contract(first_op, second_op):
    return lax.dot_general(
        first_op, second_op, (((1,), (1,)), ((), ())), preferred_element_type=jnp.float32
    )


def width_list(feature_dim):
    return [feature_dim >> WIDTHS - 1 - nested for nested in range(WIDTHS)]


def scores(first_op, second_op):
    uppers = width_list(first_op.shape[1])
    result = []
    running = jnp.zeros((first_op.shape[0], second_op.shape[0]), jnp.float32)
    lower_col = 0
    for upper_col in uppers:
        running = running + contract(
            first_op[:, lower_col:upper_col], second_op[:, lower_col:upper_col]
        )
        result.append(running * (logit_gain * upper_col ** (-0.5)))
        lower_col = upper_col
    return result


def band_sums(logit_list, total_list, target, uppers):
    bands = [None] * len(uppers)
    running = None
    for nested in reversed(range(len(uppers))):
        scale = logit_gain * uppers[nested] ** (-0.5)
        weight = (jnp.exp(logit_list[nested] - total_list[nested]) - target) * scale
        running = weight if running is None else running + weight
        bands[nested] = running.astype(jnp.bfloat16)
    return bands


def spread(bands, operand, uppers):
    pieces = []
    lower_col = 0
    for nested, upper_col in enumerate(uppers):
        block_part = operand[:, lower_col:upper_col]
        product = jnp.dot(bands[nested], block_part, preferred_element_type=jnp.float32)
        pieces.append(product)
        lower_col = upper_col
    return jnp.concatenate(pieces, axis=1)


def combine(first_pair, second_pair):
    biggest = jnp.maximum(first_pair[0], second_pair[0])
    return (
        biggest,
        first_pair[1] * jnp.exp(first_pair[0] - biggest)
        + second_pair[1] * jnp.exp(second_pair[0] - biggest),
    )


def on_device(queries, documents, partner):
    own_rows = queries.shape[0]
    uppers = width_list(queries.shape[1])
    rep_index = lax.axis_index("rep")
    dp_index = lax.axis_index("dp")
    rep_count = lax.axis_size("rep")
    every_rows = None
    every_partner = None
    every_rows, every_partner = (
        lax.all_gather(queries, ("dp", "rep"), axis=0, tiled=True),
        lax.all_gather(partner, ("dp", "rep"), axis=0, tiled=True),
    )
    pair_rows, pair_partner = (
        lax.all_gather(queries, "rep", axis=0, tiled=True),
        lax.all_gather(partner, "rep", axis=0, tiled=True),
    )
    partner_docs = lax.all_gather(documents, "dp", axis=0, tiled=True)
    col_pos = jnp.arange(partner_docs.shape[0], dtype=jnp.int32)
    col_ids = (col_pos // own_rows * rep_count + rep_index) * own_rows + col_pos % own_rows
    target = (pair_partner[:, None] == col_ids[None, :]).astype(jnp.float32)
    logit_list = scores(pair_rows, partner_docs)
    row_peaks = jnp.stack([jnp.max(logits, axis=1) for logits in logit_list])
    masses = jnp.stack(
        [
            jnp.sum(jnp.exp(logits - row_peaks[nested][:, None]), axis=1)
            for nested, logits in enumerate(logit_list)
        ]
    )
    row_peaks, masses = merged((row_peaks, masses), "rep", combine)
    totals = row_peaks + jnp.log(masses)
    bands = band_sums(
        logit_list, [totals[nested][:, None] for nested in range(len(uppers))], target, uppers
    )
    partial_queries = spread(bands, partner_docs, uppers)
    grad_queries = lax.psum_scatter(partial_queries, "rep", scatter_dimension=0, tiled=True)
    all_totals = lax.all_gather(totals, "dp", axis=1, tiled=True)
    own_ids = (dp_index * rep_count + rep_index) * own_rows + jnp.arange(own_rows, dtype=jnp.int32)
    own_target = (own_ids[:, None] == every_partner[None, :]).astype(jnp.float32)
    own_logits = scores(documents, every_rows)
    own_bands = band_sums(
        own_logits,
        [all_totals[nested][None, :] for nested in range(len(uppers))],
        own_target,
        uppers,
    )
    grad_documents = spread(own_bands, every_rows, uppers)
    return (grad_queries, grad_documents)


def solution(mesh):
    return jax.shard_map(
        on_device,
        mesh=mesh,
        in_specs=(P(("dp", "rep"), None), P(("dp", "rep"), None), P(("dp", "rep"))),
        out_specs=(P(("dp", "rep"), None), P(("dp", "rep"), None)),
        check_vma=False,
    )
```

profile of v0, /device:TPU:0, one launch (start us, length us, event | category | flops | bytes accessed | tf_op | source)
XLA Modules:
  0.0 192.3 jit_solution(15431763824458192233)
XLA Ops:
  7.2 0.0 all-gather.7.cloned.1.call-start
  7.2 0.7 all-gather.7.cloned.1.call-update
  7.9 0.0 all-gather.9.cloned.1.call-start
  7.9 0.7 all-gather.9.cloned.1.call-update
  8.6 0.0 reduce-scatter.2.cloned.1.call-start
  8.7 1.2 dynamic-slice
  10.6 0.9 dynamic-update-slice
  11.5 0.8 dynamic-update-slice.1
  12.3 2.0 %all-reduce = s32[128]{0:T(128)S(1)} all-reduce(s32[128]{0:T(128)S(1)} %dynamic-update-slice), channel_id=1, replica_groups=mesh['dp'=16,'rep'=2] {'rep'}, use_global_device_ids=true, to_apply=%add | all-reduce | flops 128 | bytes 1024
  14.3 42.2 %all-reduce.1 = s32[2048]{0:T(1024)S(1)} all-reduce(s32[2048]{0:T(1024)S(1)} %dynamic-update-slice.1), channel_id=1, replica_groups=mesh['dp'=16,'rep'=2] {'dp','rep'}, use_global_device_ids=true, to_apply=%add.1 | all-reduce | flops 2048 | bytes 16384
  56.5 2.4 %all_gather.30 = bf16[128,2048]{1,0:T(8,128)(2,1)S(1)} all-gather(bf16[64,2048]{1,0:T(8,128)(2,1)} %param.3), channel_id=1, replica_groups=mesh['dp'=16,'rep'=2] {'rep'}, dimensions={0}, use_global_device_ids=true | all-gather | bytes 786432 | tf_op jit(solution)/shard_map/all_gather | solution.py:88
  58.9 30.3 %all-gather.7.cloned.1.call-done = bf16[1024,2048]{1,0:T(8,128)(2,1)} async-done(((bf16[64,2048]{1,0:T(8,128)(2,1)}), bf16[1024,2048]{1,0:T(8,128)(2,1)}) %all-gather.7.cloned.1.call-update) | async-done | bytes 4194320 | tf_op jit(solution)/shard_map/all_gather | solution.py:91
  89.2 1.4 multiply_reduce_fusion.7
  90.7 1.5 multiply_reduce_fusion.6
  92.2 1.3 multiply_reduce_fusion.5
  93.5 1.3 multiply_reduce_fusion.4
  94.9 0.4 multiply_reduce_fusion.3
  95.3 0.3 multiply_reduce_fusion.2
  95.6 1.2 multiply_reduce_fusion.1
  96.9 1.5 multiply_reduce_fusion
  98.4 2.0 %fusion.197 = (f32[128]{0:T(128)S(1)}, f32[128,1024]{1,0:T(8,128)S(1)}) fusion(f32[128,1024]{1,0:T(8,128)S(1)} %get-tuple-element.60, bf16[1024,2048]{1,0:T(8,128)(2,1)S(1)} %copy-done.1, bf16[128,2048]{1,0:T(8,128)(2,1)} %copy-done.8), kind=kOutput, calls=%fused_computation.231 | convolution fusion | flops 268828544 | bytes 3408384 | tf_op jit(solution)/shard_map/dot_general | solution.py:21
  100.4 0.2 exponential_reduce_fusion
  100.7 0.2 exponential_reduce_fusion.8
  100.9 0.2 exponential_reduce_fusion.7
  101.1 0.2 exponential_reduce_fusion.6
  101.4 0.2 exponential_reduce_fusion.5
  101.6 0.2 exponential_reduce_fusion.4
  101.9 0.2 exponential_reduce_fusion.3
  102.1 0.2 exponential_reduce_fusion.2
  102.4 0.2 exponential_reduce_fusion.1
  102.7 1.9 %all-gather.3 = f32[2,9,128]{2,1,0:T(8,128)S(1)} all-gather(f32[1,9,128]{2,1,0:T(8,128)S(1)} %bitcast.79), channel_id=3, replica_groups=mesh['dp'=16,'rep'=2] {'rep'}, dimensions={0}, use_global_device_ids=true | all-gather | bytes 13824 | tf_op jit(solution)/shard_map/all_gather | solution.py:11
  104.6 1.8 all-gather.2
  106.5 2.2 %fusion.53 = (f32[128,1024]{1,0:T(8,128)S(1)}, f32[128,1024]{1,0:T(8,128)S(1)}, bf16[128,1024]{1,0:T(8,128)(2,1)S(1)}, f32[128,1024]{1,0:T(8,128)S(1)}) fusion(f32[128,1024]{1,0:T(8,128)S(1)} %get-tuple-element.50, f32[128]{0:T(128)S(1)} %get-tuple-element.38, s32[1024]{0:T(1024)S(1)} %fusion.177, s32[128]{0:T(128)S(1)} %all-reduce, ...), kind=kLoop, calls=%fused_computation.68 | loop fusion | flops 4718592 | bytes 5513216 | tf_op jit(solution)/shard_map/add | solution.py:50
  108.7 0.3 fusion.115
  108.9 0.3 fusion.121
  109.3 0.3 fusion.117
  109.6 0.4 fusion.119
  110.0 0.4 fusion.123
  110.4 0.4 fusion.95
  110.8 0.3 fusion.38
  111.1 0.5 fusion.130
  111.7 0.6 fusion.25
  112.2 1.3 concatenate.6
  113.5 40.8 %all_gather.38 = f32[9,2048]{1,0:T(8,128)S(1)} all-gather(f32[9,128]{1,0:T(8,128)S(1)} %fusion.165), channel_id=1, replica_groups=mesh['dp'=16,'rep'=2] {'dp'}, dimensions={1}, use_global_device_ids=true | all-gather | bytes 78336 | tf_op jit(solution)/shard_map/all_gather | solution.py:110
  154.4 14.2 %all-gather.9.cloned.1.call-done = bf16[2048,2048]{1,0:T(8,128)(2,1)} async-done(((bf16[64,2048]{1,0:T(8,128)(2,1)}), bf16[2048,2048]{1,0:T(8,128)(2,1)}) %all-gather.9.cloned.1.call-update) | async-done | bytes 8388624 | tf_op jit(solution)/shard_map/all_gather | solution.py:84
  168.6 1.5 fusion.93
  170.1 1.7 convolution_add_fusion.6
  171.8 1.4 convolution_add_fusion.5
  173.2 1.4 convolution_add_fusion.4
  174.7 1.4 convolution_add_fusion.3
  176.1 1.3 convolution_add_fusion.2
  177.4 0.4 convolution_add_fusion.1
  177.9 0.8 convolution_add_fusion
  178.7 2.0 %fusion.70 = (f32[64,2048]{1,0:T(8,128)S(1)}, f32[64,2048]{1,0:T(8,128)S(1)}, f32[64,2048]{1,0:T(8,128)S(1)}, f32[64,2048]{1,0:T(8,128)S(1)}) fusion(f32[64,2048]{1,0:T(8,128)S(1)} %convolution_add_fusion.5, f32[2048]{0:T(1024)S(1)} %bitcast.84, s32[2048]{0:T(1024)S(1)} %all-reduce.1, s32[64]{0:T(128)S(1)} %iota_add_fusion, f32[2048]{0:T(1024)S(1)} %bitcast.77, ...), kind=kOutput, calls=%fused_computation.85 | convolution fusion | flops 273285120 | bytes 9634304 | tf_op jit(solution)/shard_map/dot_general | solution.py:21
  180.7 0.4 fusion.85
  181.0 0.4 fusion.79
  181.4 0.5 fusion.82
  181.9 0.5 fusion.88
  182.3 0.4 fusion.76
  182.7 0.3 fusion.35
  183.0 0.5 fusion.91
  183.5 0.5 fusion.22
  184.1 0.8 fusion
  184.9 0.9 concatenate.7
  (31 shorter events, 0.2 us)
Async XLA Ops:
  7.2 82.1 %all-gather.7.cloned.1.call-start = ((), (), s32[]{:S(2)}) async-start(), calls=%async_computation.1 | async-start | bytes 4456448 | tf_op jit(solution)/shard_map/all_gather | solution.py:91
  7.9 160.7 %all-gather.9.cloned.1.call-start = ((), (), s32[]{:S(2)}) async-start(), calls=%async_computation.3 | async-start | bytes 8650752 | tf_op jit(solution)/shard_map/all_gather | solution.py:84
  8.6 177.2 %reduce-scatter.2.cloned.1.call-start = ((), (), s32[]{:S(2)}) async-start(), calls=%async_computation.2 | async-start | bytes 1572864 | tf_op jit(solution)/shard_map/reduce_scatter | solution.py:109
  58.9 36.8 %copy-start.8 = (bf16[128,2048]{1,0:T(8,128)(2,1)}, bf16[128,2048]{1,0:T(8,128)(2,1)S(1)}, u32[]{:S(2)}) copy-start(bf16[128,2048]{1,0:T(8,128)(2,1)S(1)} %all_gather.30) | copy-start | bytes 1572868
  89.2 5.7 %copy-start.1 = (bf16[1024,2048]{1,0:T(8,128)(2,1)S(1)}, bf16[1024,2048]{1,0:T(8,128)(2,1)}, u32[]{:S(2)}) copy-start(bf16[1024,2048]{1,0:T(8,128)(2,1)} %all-gather.7.cloned.1.call-done) | copy-start | bytes 12582916
  90.7 10.0 %copy-start.3 = (f32[128,1024]{1,0:T(8,128)}, f32[128,1024]{1,0:T(8,128)S(1)}, u32[]{:S(2)}) copy-start(f32[128,1024]{1,0:T(8,128)S(1)} %get-tuple-element.46) | copy-start | bytes 1572868
  98.4 4.0 %copy-start.5 = (f32[128,1024]{1,0:T(8,128)}, f32[128,1024]{1,0:T(8,128)S(1)}, u32[]{:S(2)}) copy-start(f32[128,1024]{1,0:T(8,128)S(1)} %get-tuple-element.60) | copy-start | bytes 1572868
  100.4 2.2 %copy-start.6 = (f32[128,1024]{1,0:T(8,128)}, f32[128,1024]{1,0:T(8,128)S(1)}, u32[]{:S(2)}) copy-start(f32[128,1024]{1,0:T(8,128)S(1)} %get-tuple-element.62) | copy-start | bytes 1572868
  102.7 6.0 %copy-start.2 = (bf16[1024,2048]{1,0:T(8,128)(2,1)S(1)}, bf16[1024,2048]{1,0:T(8,128)(2,1)}, u32[]{:S(2)}) copy-start(bf16[1024,2048]{1,0:T(8,128)(2,1)} %all-gather.7.cloned.1.call-done) | copy-start | bytes 12582916
  108.7 2.4 %copy-start.4 = (f32[128,1024]{1,0:T(8,128)S(1)}, f32[128,1024]{1,0:T(8,128)}, u32[]{:S(2)}) copy-start(f32[128,1024]{1,0:T(8,128)} %copy-done.3) | copy-start | bytes 1572868
  109.6 2.1 %copy-start.7 = (f32[128,1024]{1,0:T(8,128)S(1)}, f32[128,1024]{1,0:T(8,128)}, u32[]{:S(2)}) copy-start(f32[128,1024]{1,0:T(8,128)} %copy-done.6) | copy-start | bytes 1572868
  111.1 57.5 %copy-start.9 = (bf16[64,2048]{1,0:T(8,128)(2,1)S(1)}, bf16[64,2048]{1,0:T(8,128)(2,1)}, u32[]{:S(2)}) copy-start(bf16[64,2048]{1,0:T(8,128)(2,1)} %param.4) | copy-start | bytes 786436
  168.6 8.8 %copy-start = (bf16[2048,2048]{1,0:T(8,128)(2,1)S(1)}, bf16[2048,2048]{1,0:T(8,128)(2,1)}, u32[]{:S(2)}) copy-start(bf16[2048,2048]{1,0:T(8,128)(2,1)} %all-gather.9.cloned.1.call-done) | copy-start | bytes 25165828
Sparse Core Ops, SparseCore 0:
  10.7 78.4 all-gather.6
  92.1 76.4 all-gather.8
  171.4 7.1 reduce-scatter.1
where the time goes:
time: 193 us; the launch traced here: 192 us
  blocking collectives  91.1 us (47%)
  waiting for transfers between devices  46 us (24%)
  matrix products  30.8 us (16%)
  between operations  14.7 us (8%)
  local copies, waits for them, and re-layouts  5.31 us (3%)
  other arithmetic  4.33 us (2%)
    unnamed x2, blocking collectives  44.2 us
    all_gather x1, blocking collectives, on_device(): all_totals = lax.all_gather(totals, 'dp', axis=1, tiled=True)  40.8 us
    all_gather x1, waiting for transfers between devices, on_device(): partner_docs = lax.all_gather(documents, 'dp', axis=0, tiled=True)  30.3 us
    dot_general x18, matrix products, contract(): lax.dot_general(first_op, second_op, (((1,), (1,)), ((), ())), preferred_...  23.2 us
    all_gather x1, waiting for transfers between devices, on_device(): lax.all_gather(queries, ('dp', 'rep'), axis=0, tiled=True)  14.2 us
    dot_general x18, matrix products, spread(): jnp.dot(bands[nested], block_part, preferred_element_type=jnp.float32)  7.64 us
  transfers between devices with their start and end apart: 3, of which 2 were waited for; matrix products, arithmetic and copies ran while one was open for 21% of the time, Pallas kernels for 0%

commit v1 on v0

--- a/solution.py
+++ b/solution.py
@@ -107,7 +107,12 @@
     )
     partial_queries = spread(bands, partner_docs, uppers)
     grad_queries = lax.psum_scatter(partial_queries, "rep", scatter_dimension=0, tiled=True)
-    all_totals = lax.all_gather(totals, "dp", axis=1, tiled=True)
+    ring = [totals]
+    for hop_ in range(15):
+        ring.append(lax.ppermute(ring[-1], "dp", [(dev, (dev + 1) % 16) for dev in range(16)]))
+    all_totals = jnp.roll(
+        jnp.concatenate(ring[::-1], axis=1), (lax.axis_index("dp") + 1) * ring[0].shape[1], axis=1
+    )
     own_ids = (dp_index * rep_count + rep_index) * own_rows + jnp.arange(own_rows, dtype=jnp.int32)
     own_target = (own_ids[:, None] == every_partner[None, :]).astype(jnp.float32)
     own_logits = scores(documents, every_rows)

time: 193 us -> 280 us (1.45)
  waiting for transfers between devices: 46 us -> 170 us
  blocking collectives: 91.1 us -> 50.4 us
  starting transfers between devices: 0.11 us -> 3.93 us
    ppermute x0 -> x15, waiting for transfers between devices: none -> 91 us  [on_device(): lax.ppermute(ring[-1], 'dp', [(dev, (dev + 1) % 16) for dev in range(16)])]
    all_gather x1, waiting for transfers between devices: 30.3 us -> 77.9 us  [on_device(): partner_docs = lax.all_gather(documents, 'dp', axis=0, tiled=True)]
    all_gather x1 -> x0, blocking collectives: 40.8 us -> none  [on_device(): all_totals = lax.all_gather(totals, 'dp', axis=1, tiled=True)]
    all_gather x1, waiting for transfers between devices: 14.2 us -> 0.02 us  [on_device(): lax.all_gather(queries, ('dp', 'rep'), axis=0, tiled=True)]
    ppermute x0 -> x15, starting transfers between devices: none -> 3.81 us  [on_device(): lax.ppermute(ring[-1], 'dp', [(dev, (dev + 1) % 16) for dev in range(16)])]
  transfers between devices with their start and end apart: 3 -> 18, of which waited for: 2 -> 15; matrix products, arithmetic and copies ran while one was open for 21% -> 14% of each run, Pallas kernels for 0% -> 0%
where the time goes in v1:
time: 280 us; the launch traced here: 279 us
  waiting for transfers between devices  170 us (61%)
  blocking collectives  50.4 us (18%)
  matrix products  31.4 us (11%)
  between operations  14.9 us (5%)
  other arithmetic  4.39 us (2%)
  starting transfers between devices  3.93 us (1%)
  local copies, waits for them, and re-layouts  3.73 us (1%)
    ppermute x15, waiting for transfers between devices, on_device(): lax.ppermute(ring[-1], 'dp', [(dev, (dev + 1) % 16) for dev in range(16)])  91 us
    all_gather x1, waiting for transfers between devices, on_device(): partner_docs = lax.all_gather(documents, 'dp', axis=0, tiled=True)  77.9 us
    unnamed x2, blocking collectives  44.3 us
    dot_general x18, matrix products, contract(): lax.dot_general(first_op, second_op, (((1,), (1,)), ((), ())), preferred_...  23.6 us
    dot_general x18, matrix products, spread(): jnp.dot(bands[nested], block_part, preferred_element_type=jnp.float32)  7.8 us
  transfers between devices with their start and end apart: 18, of which 15 were waited for; matrix products, arithmetic and copies ran while one was open for 14% of the time, Pallas kernels for 0%

profile of v1, /device:TPU:0, one launch (start us, length us, event | category | flops | bytes accessed | tf_op | source)
XLA Modules:
  0.0 279.1 jit_solution(6944885233646773451)
XLA Ops:
  7.2 0.7 all-gather.7.cloned.1.call-update
  7.9 0.7 all-gather.9.cloned.1.call-update
  8.7 2.5 all_gather.27
  11.2 77.9 %all-gather.7.cloned.1.call-done = bf16[1024,2048]{1,0:T(8,128)(2,1)} async-done(((bf16[64,2048]{1,0:T(8,128)(2,1)}), bf16[1024,2048]{1,0:T(8,128)(2,1)}) %all-gather.7.cloned.1.call-update) | async-done | bytes 4194320 | tf_op jit(solution)/shard_map/all_gather | solution.py:91
  89.1 1.4 multiply_reduce_fusion.7
  90.5 1.5 multiply_reduce_fusion.6
  92.1 1.4 multiply_reduce_fusion.5
  93.4 1.4 multiply_reduce_fusion.4
  94.8 0.4 multiply_reduce_fusion.3
  95.2 0.3 multiply_reduce_fusion.2
  95.5 1.2 multiply_reduce_fusion.1
  96.8 1.5 multiply_reduce_fusion
  98.3 2.1 fusion.192
  102.6 1.8 all-gather.3
  104.4 1.8 all-gather.2
  106.2 1.5 collective-permute-start
  107.7 5.9 %collective-permute-done = f32[9,128]{1,0:T(8,128)S(1)} collective-permute-done((f32[9,128]{1,0:T(8,128)S(1)}, f32[9,128]{1,0:T(8,128)S(1)}, u32[]{:S(2)}, u32[]{:S(2)}) %collective-permute-start) | collective-permute-done | bytes 4640 | tf_op jit(solution)/shard_map/ppermute | solution.py:112
  113.6 7.3 %collective-permute-done.1 = f32[9,128]{1,0:T(8,128)S(1)} collective-permute-done((f32[9,128]{1,0:T(8,128)S(1)}, f32[9,128]{1,0:T(8,128)S(1)}, u32[]{:S(2)}, u32[]{:S(2)}) %collective-permute-start.1) | collective-permute-done | bytes 4640 | tf_op jit(solution)/shard_map/ppermute | solution.py:112
  121.0 7.4 %collective-permute-done.2 = f32[9,128]{1,0:T(8,128)S(1)} collective-permute-done((f32[9,128]{1,0:T(8,128)S(1)}, f32[9,128]{1,0:T(8,128)S(1)}, u32[]{:S(2)}, u32[]{:S(2)}) %collective-permute-start.2) | collective-permute-done | bytes 4640 | tf_op jit(solution)/shard_map/ppermute | solution.py:112
  128.4 0.6 dynamic-slice
  130.2 1.8 all-reduce
  132.0 42.5 %all-reduce.1 = s32[2048]{0:T(1024)S(1)} all-reduce(s32[2048]{0:T(1024)S(1)} %dynamic-update-slice.1), channel_id=1, replica_groups=mesh['dp'=16,'rep'=2] {'dp','rep'}, use_global_device_ids=true, to_apply=%add.1 | all-reduce | flops 2048 | bytes 16384
  174.5 2.3 collective-permute-start.4
  176.8 5.0 %collective-permute-done.4 = f32[9,128]{1,0:T(8,128)S(1)} collective-permute-done((f32[9,128]{1,0:T(8,128)S(1)}, f32[9,128]{1,0:T(8,128)S(1)}, u32[]{:S(2)}, u32[]{:S(2)}) %collective-permute-start.4) | collective-permute-done | bytes 4640 | tf_op jit(solution)/shard_map/ppermute | solution.py:112
  181.8 2.2 fusion.41
  184.0 5.0 %collective-permute-done.5 = f32[9,128]{1,0:T(8,128)S(1)} collective-permute-done((f32[9,128]{1,0:T(8,128)S(1)}, f32[9,128]{1,0:T(8,128)S(1)}, u32[]{:S(2)}, u32[]{:S(2)}) %collective-permute-start.5) | collective-permute-done | bytes 4640 | tf_op jit(solution)/shard_map/ppermute | solution.py:112
  189.0 0.6 fusion.13
  189.6 6.7 %collective-permute-done.6 = f32[9,128]{1,0:T(8,128)S(1)} collective-permute-done((f32[9,128]{1,0:T(8,128)S(1)}, f32[9,128]{1,0:T(8,128)S(1)}, u32[]{:S(2)}, u32[]{:S(2)}) %collective-permute-start.6) | collective-permute-done | bytes 4640 | tf_op jit(solution)/shard_map/ppermute | solution.py:112
  196.3 0.5 fusion.124
  196.8 6.7 %collective-permute-done.7 = f32[9,128]{1,0:T(8,128)S(1)} collective-permute-done((f32[9,128]{1,0:T(8,128)S(1)}, f32[9,128]{1,0:T(8,128)S(1)}, u32[]{:S(2)}, u32[]{:S(2)}) %collective-permute-start.7) | collective-permute-done | bytes 4640 | tf_op jit(solution)/shard_map/ppermute | solution.py:112
  203.5 0.3 fusion.26
  203.8 6.9 %collective-permute-done.8 = f32[9,128]{1,0:T(8,128)S(1)} collective-permute-done((f32[9,128]{1,0:T(8,128)S(1)}, f32[9,128]{1,0:T(8,128)S(1)}, u32[]{:S(2)}, u32[]{:S(2)}) %collective-permute-start.8) | collective-permute-done | bytes 4640 | tf_op jit(solution)/shard_map/ppermute | solution.py:112
  210.8 0.4 fusion.84
  211.1 6.9 %collective-permute-done.9 = f32[9,128]{1,0:T(8,128)S(1)} collective-permute-done((f32[9,128]{1,0:T(8,128)S(1)}, f32[9,128]{1,0:T(8,128)S(1)}, u32[]{:S(2)}, u32[]{:S(2)}) %collective-permute-start.9) | collective-permute-done | bytes 4640 | tf_op jit(solution)/shard_map/ppermute | solution.py:112
  218.0 0.4 fusion.116
  218.4 6.8 %collective-permute-done.10 = f32[9,128]{1,0:T(8,128)S(1)} collective-permute-done((f32[9,128]{1,0:T(8,128)S(1)}, f32[9,128]{1,0:T(8,128)S(1)}, u32[]{:S(2)}, u32[]{:S(2)}) %collective-permute-start.10) | collective-permute-done | bytes 4640 | tf_op jit(solution)/shard_map/ppermute | solution.py:112
  225.3 0.4 fusion.112
  225.7 6.8 %collective-permute-done.11 = f32[9,128]{1,0:T(8,128)S(1)} collective-permute-done((f32[9,128]{1,0:T(8,128)S(1)}, f32[9,128]{1,0:T(8,128)S(1)}, u32[]{:S(2)}, u32[]{:S(2)}) %collective-permute-start.11) | collective-permute-done | bytes 4640 | tf_op jit(solution)/shard_map/ppermute | solution.py:112
  232.5 0.3 fusion.114
  232.8 6.9 %collective-permute-done.12 = f32[9,128]{1,0:T(8,128)S(1)} collective-permute-done((f32[9,128]{1,0:T(8,128)S(1)}, f32[9,128]{1,0:T(8,128)S(1)}, u32[]{:S(2)}, u32[]{:S(2)}) %collective-permute-start.12) | collective-permute-done | bytes 4640 | tf_op jit(solution)/shard_map/ppermute | solution.py:112
  239.7 0.3 fusion.110
  240.1 6.9 %collective-permute-done.13 = f32[9,128]{1,0:T(8,128)S(1)} collective-permute-done((f32[9,128]{1,0:T(8,128)S(1)}, f32[9,128]{1,0:T(8,128)S(1)}, u32[]{:S(2)}, u32[]{:S(2)}) %collective-permute-start.13) | collective-permute-done | bytes 4640 | tf_op jit(solution)/shard_map/ppermute | solution.py:112
  247.0 0.3 fusion.108
  247.3 1.3 concatenate.12
  248.6 5.7 %collective-permute-done.14 = f32[9,128]{1,0:T(8,128)S(1)} collective-permute-done((f32[9,128]{1,0:T(8,128)S(1)}, f32[9,128]{1,0:T(8,128)S(1)}, u32[]{:S(2)}, u32[]{:S(2)}) %collective-permute-start.14) | collective-permute-done | bytes 4640 | tf_op jit(solution)/shard_map/ppermute | solution.py:112
  254.8 1.5 fusion.82
  256.4 2.1 convolution_add_fusion.6
  258.5 1.4 convolution_add_fusion.5
  259.9 1.4 convolution_add_fusion.4
  261.3 1.4 convolution_add_fusion.3
  262.7 1.3 convolution_add_fusion.2
  264.1 0.4 convolution_add_fusion.1
  264.5 0.8 convolution_add_fusion
  265.3 2.0 fusion.59
  267.3 0.4 fusion.74
  267.6 0.4 fusion.68
  268.0 0.5 fusion.71
  268.5 0.5 fusion.77
  269.0 0.4 fusion.65
  269.4 0.3 fusion.23
  269.7 0.5 fusion.80
  270.1 0.7 fusion.10
  270.8 0.9 fusion
  271.7 0.9 concatenate.14
  (96 shorter events, 3.3 us)
Async XLA Ops:
  7.2 81.9 %all-gather.7.cloned.1.call-start = ((), (), s32[]{:S(2)}) async-start(), calls=%async_computation.1 | async-start | bytes 4456448 | tf_op jit(solution)/shard_map/all_gather | solution.py:91
  7.9 246.9 %all-gather.9.cloned.1.call-start = ((), (), s32[]{:S(2)}) async-start(), calls=%async_computation.3 | async-start | bytes 8650752 | tf_op jit(solution)/shard_map/all_gather | solution.py:84
  8.6 264.0 %reduce-scatter.2.cloned.1.call-start = ((), (), s32[]{:S(2)}) async-start(), calls=%async_computation.2 | async-start | bytes 1572864 | tf_op jit(solution)/shard_map/reduce_scatter | solution.py:109
  11.2 84.3 %copy-start.8 = (bf16[128,2048]{1,0:T(8,128)(2,1)}, bf16[128,2048]{1,0:T(8,128)(2,1)S(1)}, u32[]{:S(2)}) copy-start(bf16[128,2048]{1,0:T(8,128)(2,1)S(1)} %all_gather.27) | copy-start | bytes 1572868
  89.1 5.7 %copy-start.1 = (bf16[1024,2048]{1,0:T(8,128)(2,1)S(1)}, bf16[1024,2048]{1,0:T(8,128)(2,1)}, u32[]{:S(2)}) copy-start(bf16[1024,2048]{1,0:T(8,128)(2,1)} %all-gather.7.cloned.1.call-done) | copy-start | bytes 12582916
  90.5 10.1 %copy-start.3 = (f32[128,1024]{1,0:T(8,128)}, f32[128,1024]{1,0:T(8,128)S(1)}, u32[]{:S(2)}) copy-start(f32[128,1024]{1,0:T(8,128)S(1)} %get-tuple-element.46) | copy-start | bytes 1572868
  98.2 4.0 %copy-start.5 = (f32[128,1024]{1,0:T(8,128)}, f32[128,1024]{1,0:T(8,128)S(1)}, u32[]{:S(2)}) copy-start(f32[128,1024]{1,0:T(8,128)S(1)} %get-tuple-element.60) | copy-start | bytes 1572868
  98.2 30.2 %copy-start.11 = (u32[32]{0:T(128)S(1)}, u32[32]{0:T(128)}, u32[]{:S(2)}) copy-start(u32[32]{0:T(128)} %constant.109) | copy-start | bytes 388
  98.3 31.4 %copy-start.10 = (s32[64]{0:T(128)S(1)}, s32[64]{0:T(128)}, u32[]{:S(2)}) copy-start(s32[64]{0:T(128)} %param.5) | copy-start | bytes 772
  100.3 2.2 copy-start.6
  106.2 7.4 %collective-permute-start = (f32[9,128]{1,0:T(8,128)S(1)}, f32[9,128]{1,0:T(8,128)S(1)}, u32[]{:S(2)}, u32[]{:S(2)}) collective-permute-start(f32[9,128]{1,0:T(8,128)S(1)} %fusion.159), channel_id=1, source_target_pairs={{0,2},{2,4},{4,6},{6,8},{8,10},{10,12},{12,14},{14,16},{16,18},{18... | collective-permute-start | bytes 13832 | tf_op jit(solution)/shard_map/ppermute | solution.py:112
  113.6 7.4 %collective-permute-start.1 = (f32[9,128]{1,0:T(8,128)S(1)}, f32[9,128]{1,0:T(8,128)S(1)}, u32[]{:S(2)}, u32[]{:S(2)}) collective-permute-start(f32[9,128]{1,0:T(8,128)S(1)} %collective-permute-done), channel_id=1, source_target_pairs={{0,2},{2,4},{4,6},{6,8},{8,10},{10,12},{12,14},{14,16},{16,18},{18... | collective-permute-start | bytes 13832 | tf_op jit(solution)/shard_map/ppermute | solution.py:112
  121.0 7.5 %collective-permute-start.2 = (f32[9,128]{1,0:T(8,128)S(1)}, f32[9,128]{1,0:T(8,128)S(1)}, u32[]{:S(2)}, u32[]{:S(2)}) collective-permute-start(f32[9,128]{1,0:T(8,128)S(1)} %collective-permute-done.1), channel_id=1, source_target_pairs={{0,2},{2,4},{4,6},{6,8},{8,10},{10,12},{12,14},{14,16},{16,18},{18... | collective-permute-start | bytes 13832 | tf_op jit(solution)/shard_map/ppermute | solution.py:112
  128.4 46.1 %collective-permute-start.3 = (f32[9,128]{1,0:T(8,128)S(1)}, f32[9,128]{1,0:T(8,128)S(1)}, u32[]{:S(2)}, u32[]{:S(2)}) collective-permute-start(f32[9,128]{1,0:T(8,128)S(1)} %collective-permute-done.2), channel_id=1, source_target_pairs={{0,2},{2,4},{4,6},{6,8},{8,10},{10,12},{12,14},{14,16},{16,18},{18... | collective-permute-start | bytes 13832 | tf_op jit(solution)/shard_map/ppermute | solution.py:112
  174.5 14.6 %copy-start.2 = (bf16[1024,2048]{1,0:T(8,128)(2,1)S(1)}, bf16[1024,2048]{1,0:T(8,128)(2,1)}, u32[]{:S(2)}) copy-start(bf16[1024,2048]{1,0:T(8,128)(2,1)} %all-gather.7.cloned.1.call-done) | copy-start | bytes 12582916
  174.5 14.6 %copy-start.7 = (f32[128,1024]{1,0:T(8,128)S(1)}, f32[128,1024]{1,0:T(8,128)}, u32[]{:S(2)}) copy-start(f32[128,1024]{1,0:T(8,128)} %copy-done.6) | copy-start | bytes 1572868
  174.5 7.3 %collective-permute-start.4 = (f32[9,128]{1,0:T(8,128)S(1)}, f32[9,128]{1,0:T(8,128)S(1)}, u32[]{:S(2)}, u32[]{:S(2)}) collective-permute-start(f32[9,128]{1,0:T(8,128)S(1)} %collective-permute-done.3), channel_id=1, source_target_pairs={{0,2},{2,4},{4,6},{6,8},{8,10},{10,12},{12,14},{14,16},{16,18},{18... | collective-permute-start | bytes 13832 | tf_op jit(solution)/shard_map/ppermute | solution.py:112
  181.8 7.2 %collective-permute-start.5 = (f32[9,128]{1,0:T(8,128)S(1)}, f32[9,128]{1,0:T(8,128)S(1)}, u32[]{:S(2)}, u32[]{:S(2)}) collective-permute-start(f32[9,128]{1,0:T(8,128)S(1)} %collective-permute-done.4), channel_id=1, source_target_pairs={{0,2},{2,4},{4,6},{6,8},{8,10},{10,12},{12,14},{14,16},{16,18},{18... | collective-permute-start | bytes 13832 | tf_op jit(solution)/shard_map/ppermute | solution.py:112
  181.8 14.5 %copy-start.4 = (f32[128,1024]{1,0:T(8,128)S(1)}, f32[128,1024]{1,0:T(8,128)}, u32[]{:S(2)}) copy-start(f32[128,1024]{1,0:T(8,128)} %copy-done.3) | copy-start | bytes 1572868
  189.0 7.2 %collective-permute-start.6 = (f32[9,128]{1,0:T(8,128)S(1)}, f32[9,128]{1,0:T(8,128)S(1)}, u32[]{:S(2)}, u32[]{:S(2)}) collective-permute-start(f32[9,128]{1,0:T(8,128)S(1)} %collective-permute-done.5), channel_id=1, source_target_pairs={{0,2},{2,4},{4,6},{6,8},{8,10},{10,12},{12,14},{14,16},{16,18},{18... | collective-permute-start | bytes 13832 | tf_op jit(solution)/shard_map/ppermute | solution.py:112
  196.3 7.2 %collective-permute-start.7 = (f32[9,128]{1,0:T(8,128)S(1)}, f32[9,128]{1,0:T(8,128)S(1)}, u32[]{:S(2)}, u32[]{:S(2)}) collective-permute-start(f32[9,128]{1,0:T(8,128)S(1)} %collective-permute-done.6), channel_id=1, source_target_pairs={{0,2},{2,4},{4,6},{6,8},{8,10},{10,12},{12,14},{14,16},{16,18},{18... | collective-permute-start | bytes 13832 | tf_op jit(solution)/shard_map/ppermute | solution.py:112
  203.5 7.2 %collective-permute-start.8 = (f32[9,128]{1,0:T(8,128)S(1)}, f32[9,128]{1,0:T(8,128)S(1)}, u32[]{:S(2)}, u32[]{:S(2)}) collective-permute-start(f32[9,128]{1,0:T(8,128)S(1)} %collective-permute-done.7), channel_id=1, source_target_pairs={{0,2},{2,4},{4,6},{6,8},{8,10},{10,12},{12,14},{14,16},{16,18},{18... | collective-permute-start | bytes 13832 | tf_op jit(solution)/shard_map/ppermute | solution.py:112
  210.8 7.2 %collective-permute-start.9 = (f32[9,128]{1,0:T(8,128)S(1)}, f32[9,128]{1,0:T(8,128)S(1)}, u32[]{:S(2)}, u32[]{:S(2)}) collective-permute-start(f32[9,128]{1,0:T(8,128)S(1)} %collective-permute-done.8), channel_id=1, source_target_pairs={{0,2},{2,4},{4,6},{6,8},{8,10},{10,12},{12,14},{14,16},{16,18},{18... | collective-permute-start | bytes 13832 | tf_op jit(solution)/shard_map/ppermute | solution.py:112
  218.0 7.2 %collective-permute-start.10 = (f32[9,128]{1,0:T(8,128)S(1)}, f32[9,128]{1,0:T(8,128)S(1)}, u32[]{:S(2)}, u32[]{:S(2)}) collective-permute-start(f32[9,128]{1,0:T(8,128)S(1)} %collective-permute-done.9), channel_id=1, source_target_pairs={{0,2},{2,4},{4,6},{6,8},{8,10},{10,12},{12,14},{14,16},{16,18},{18... | collective-permute-start | bytes 13832 | tf_op jit(solution)/shard_map/ppermute | solution.py:112
  218.4 36.4 %copy-start.9 = (bf16[64,2048]{1,0:T(8,128)(2,1)S(1)}, bf16[64,2048]{1,0:T(8,128)(2,1)}, u32[]{:S(2)}) copy-start(bf16[64,2048]{1,0:T(8,128)(2,1)} %param.4) | copy-start | bytes 786436
  225.3 7.2 %collective-permute-start.11 = (f32[9,128]{1,0:T(8,128)S(1)}, f32[9,128]{1,0:T(8,128)S(1)}, u32[]{:S(2)}, u32[]{:S(2)}) collective-permute-start(f32[9,128]{1,0:T(8,128)S(1)} %collective-permute-done.10), channel_id=1, source_target_pairs={{0,2},{2,4},{4,6},{6,8},{8,10},{10,12},{12,14},{14,16},{16,18},{18... | collective-permute-start | bytes 13832 | tf_op jit(solution)/shard_map/ppermute | solution.py:112
  232.5 7.2 %collective-permute-start.12 = (f32[9,128]{1,0:T(8,128)S(1)}, f32[9,128]{1,0:T(8,128)S(1)}, u32[]{:S(2)}, u32[]{:S(2)}) collective-permute-start(f32[9,128]{1,0:T(8,128)S(1)} %collective-permute-done.11), channel_id=1, source_target_pairs={{0,2},{2,4},{4,6},{6,8},{8,10},{10,12},{12,14},{14,16},{16,18},{18... | collective-permute-start | bytes 13832 | tf_op jit(solution)/shard_map/ppermute | solution.py:112
  239.7 7.2 %collective-permute-start.13 = (f32[9,128]{1,0:T(8,128)S(1)}, f32[9,128]{1,0:T(8,128)S(1)}, u32[]{:S(2)}, u32[]{:S(2)}) collective-permute-start(f32[9,128]{1,0:T(8,128)S(1)} %collective-permute-done.12), channel_id=1, source_target_pairs={{0,2},{2,4},{4,6},{6,8},{8,10},{10,12},{12,14},{14,16},{16,18},{18... | collective-permute-start | bytes 13832 | tf_op jit(solution)/shard_map/ppermute | solution.py:112
  247.0 7.2 %collective-permute-start.14 = (f32[9,128]{1,0:T(8,128)S(1)}, f32[9,128]{1,0:T(8,128)S(1)}, u32[]{:S(2)}, u32[]{:S(2)}) collective-permute-start(f32[9,128]{1,0:T(8,128)S(1)} %collective-permute-done.13), channel_id=1, source_target_pairs={{0,2},{2,4},{4,6},{6,8},{8,10},{10,12},{12,14},{14,16},{16,18},{18... | collective-permute-start | bytes 13832 | tf_op jit(solution)/shard_map/ppermute | solution.py:112
  254.8 9.3 %copy-start = (bf16[2048,2048]{1,0:T(8,128)(2,1)S(1)}, bf16[2048,2048]{1,0:T(8,128)(2,1)}, u32[]{:S(2)}) copy-start(bf16[2048,2048]{1,0:T(8,128)(2,1)} %all-gather.9.cloned.1.call-done) | copy-start | bytes 25165828
Sparse Core Ops, SparseCore 0:
  10.7 78.3 all-gather.6
  91.9 76.7 all-gather.8
  248.7 9.7 reduce-scatter.1
